TPU v7x, 32 devices: a whole 2x2x4 slice. The times are simulated.
32 devices in a mesh: img: 2 (over x), rows: 16 (over z, y, core).
Axes of the slice: x: 2, y: 2, z: 4, core: 2. Of those that a mesh axis runs over, the one named last changes fastest.
Arguments:
- hidden_states: bfloat16 [3, 4096, 1024], P(None, ('img', 'rows')), parts along dimension 1, may hold values from -6 to 6
- cell_of: int32 [2048], replicated, may hold values from 0 to 2047, as said below
- proj_four_weight: bfloat16 [1024, 256], replicated, may hold values from -0.1875 to 0.1875
- proj_four_bias: float32 [256], replicated, may hold values from -3 to 3
- proj_two_weight: bfloat16 [1024, 512], replicated, may hold values from -0.1875 to 0.1875
- proj_two_bias: float32 [512], replicated, may hold values from -3 to 3
- proj_same_weight: bfloat16 [1024, 1024], replicated, may hold values from -0.1875 to 0.1875
- proj_same_bias: float32 [1024], replicated, may hold values from -3 to 3
- up4_weight: bfloat16 [256, 4096], replicated, may hold values from -0.375 to 0.375
- up4_bias: float32 [256], replicated, may hold values from -3 to 3
- up2_weight: bfloat16 [512, 2048], replicated, may hold values from -0.25 to 0.25
- up2_bias: float32 [512], replicated, may hold values from -3 to 3
- join_weight: bfloat16 [3, 3, 256, 256], replicated, may hold values from -0.125 to 0.125
Outputs:
- joined_four: bfloat16 [256, 256, 256], P(('img', 'rows')), parts along dimension 0
- upsampled_two: bfloat16 [128, 128, 512], P(('img', 'rows')), parts along dimension 0
- same_scale: bfloat16 [64, 64, 1024], P(('img', 'rows')), parts along dimension 0
There are 2 independent parts, one for each index of `img`. A program takes and returns all parts, laid end to end along the dimension named above; an argument that names none is the same for every part. Nothing has to cross between parts.
Inputs may be any that keep to these rules, and one draw needn't show every extreme that they name: `cell_of`: a permutation of the cells 0 to 2047; the sequence positions k * 128 to (k + 1) * 128 - 1 hold exactly 8 cells of every block of 128 consecutive cells.
All inputs are finite; a program needn't handle non-finite values.
Results may differ from a plain program's by a relative error of at most 0.0057.
Values may be sent and summed in bfloat16 or wider, within the bound.
A program may use at most 64 MiB of HBM per device.

v0:
```python
import functools

import jax
import jax.numpy as jnp
from jax import lax
from jax.experimental import pallas as pl
from jax.experimental.pallas import tpu as pltpu
from jax.sharding import PartitionSpec as P

GRID_W = 64
MESH = pl.DeviceIdType.MESH


def partner(me, step):
    other = me
    bit = 1
    while bit <= step:
        if step & bit:
            other = other + bit * (1 - 2 * lax.rem(lax.div(me, bit), 2))
        bit *= 2
    return other


def dot(left, right):
    return jnp.dot(left, right, preferred_element_type=jnp.float32)


def kernel(
    shards,
    hid_hbm,
    table_hbm,
    w_four_hbm,
    b_four_hbm,
    w_two_hbm,
    b_two_hbm,
    w_same_hbm,
    b_same_hbm,
    up4_hbm,
    up4_b_hbm,
    up2_hbm,
    up2_b_hbm,
    join_hbm,
    joined_ref,
    two_ref,
    same_rows_ref,
    place_ref,
    hid,
    table,
    w_four,
    b_four,
    w_two,
    b_two,
    w_same,
    b_same,
    up4,
    up4_b,
    up2,
    up2_b,
    join,
    stage,
    send_four,
    send_two,
    send_same,
    recv_four,
    recv_two,
    recv_same,
    edge_out,
    edge_in,
    planes,
    joined_f32,
    two_f32,
    load_sem,
    send_sem,
    recv_sem,
    halo_send_sem,
    halo_recv_sem,
):
    me = lax.axis_index("rows")
    img = lax.axis_index("img")
    tok = hid.shape[1]
    per = tok // shards
    rows = tok // GRID_W
    steps = list(range(1, shards))


    names = (
        (table_hbm, table),
        (hid_hbm.at[0], hid.at[0]),
        (w_four_hbm, w_four),
        (b_four_hbm, b_four),
        (hid_hbm.at[1], hid.at[1]),
        (w_two_hbm, w_two),
        (b_two_hbm, b_two),
        (hid_hbm.at[2], hid.at[2]),
        (w_same_hbm, w_same),
        (b_same_hbm, b_same),
        (up4_hbm, up4),
        (up4_b_hbm, up4_b),
        (join_hbm, join),
        (up2_hbm, up2),
        (up2_b_hbm, up2_b),
    )
    loads = [pltpu.make_async_copy(src, dst, load_sem.at[i]) for i, (src, dst) in enumerate(names)]

    for load in loads[:4]:
        load.start()

    barrier = pltpu.get_barrier_semaphore()
    for step in steps:
        pl.semaphore_signal(barrier, inc=1, device_id=(img, partner(me, step)), device_id_type=MESH)

    loads[0].wait()
    mine = jnp.broadcast_to(table[pl.ds(me, 1), :].astype(jnp.float32), (tok, tok))
    smaller = (mine.T < mine).astype(jnp.float32)
    slot_row = jnp.sum(smaller, axis=0, keepdims=True)
    down = lax.broadcasted_iota(jnp.int32, (tok, tok), 0)
    across = lax.broadcasted_iota(jnp.int32, (tok, tok), 1)
    scatter = (down.astype(jnp.float32) == slot_row).astype(jnp.float32).astype(jnp.bfloat16)

    def project(hook, first, weight, bias, send):
        channels = weight.shape[1]
        for load in loads[first : first + 3]:
            load.wait()
        projected = (dot(hid[hook], weight[...]) + bias[...]).astype(jnp.bfloat16)
        stage[:, :channels] = dot(scatter, projected)
        if first == 1:
            for load in loads[4:]:
                load.start()
        for shard in range(shards):
            send[shard] = stage[shard * per : (shard + 1) * per, :channels].astype(jnp.bfloat16)

    def exchange(index, send, recv, some):
        for step in some:
            other = partner(me, step)
            pltpu.make_async_remote_copy(
                src_ref=send.at[other],
                dst_ref=recv.at[me],
                send_sem=send_sem.at[index],
                recv_sem=recv_sem.at[index],
                device_id=(img, other),
                device_id_type=MESH,
            ).start()

    def bulk_wait(buffer, sem):
        part = buffer.at[pl.ds(0, shards - 1)]
        pltpu.make_async_copy(part, part, sem).wait()

    def collect(index, recv):
        channels = recv.shape[2]
        bulk_wait(recv, recv_sem.at[index])
        for shard in range(shards):
            stage[shard * per : (shard + 1) * per, :channels] = recv[shard].astype(jnp.float32)
        return stage[:, :channels].astype(jnp.bfloat16)

    project(0, 1, w_four, b_four, send_four)
    pl.semaphore_wait(barrier, shards - 1)
    exchange(0, send_four, recv_four, steps)
    recv_four[me] = send_four[me]
    project(1, 4, w_two, b_two, send_two)
    exchange(1, send_two, recv_two, steps)
    recv_two[me] = send_two[me]
    project(2, 7, w_same, b_same, send_same)
    far = len(steps) * 3 // 4
    exchange(2, send_same, recv_same, steps[:far])
    recv_same[me] = send_same[me]

    wanted = down + me * tok
    source = jnp.zeros((tok, tok), jnp.float32)
    for shard in range(1, shards):
        source = source + jnp.where(table[shard : shard + 1, :] == wanted, float(shard), 0.0)
    source = jnp.broadcast_to(jnp.sum(source, axis=1, keepdims=True), (tok, tok))
    earlier = jnp.where((source == source.T) & (across < down), 1.0, 0.0)
    slot_col = source * per + jnp.sum(earlier, axis=1, keepdims=True)
    place = (across.astype(jnp.float32) == slot_col).astype(jnp.float32).astype(jnp.bfloat16)
    place_ref[...] = place

    tile_four = dot(place, collect(0, recv_four)).astype(jnp.bfloat16)
    edge_out[0] = tile_four[:GRID_W]
    edge_out[1] = tile_four[tok - GRID_W :]

    def halo(side):
        return pltpu.make_async_remote_copy(
            src_ref=edge_out.at[1 - side],
            dst_ref=edge_in.at[side],
            send_sem=halo_send_sem.at[side],
            recv_sem=halo_recv_sem.at[side],
            device_id=(img, me + 1 if side == 0 else me - 1),
            device_id_type=MESH,
        )

    has_below = me < shards - 1
    has_above = me > 0

    @pl.when(has_below)
    def _():
        halo(0).start()

    @pl.when(has_above)
    def _():
        halo(1).start()

    exchange(2, send_same, recv_same, steps[far:])

    column = lax.broadcasted_iota(jnp.int32, (GRID_W, 1), 0)
    c_up = join.shape[0] // 9

    def put_row(row, phase, values):
        where = pl.ds((row + 1) * GRID_W, GRID_W)
        planes[phase + 1, where, :] = values.astype(jnp.bfloat16)
        if phase == 3:
            moved = jnp.where(column == 0, 0.0, pltpu.roll(values, 1, axis=0))
            planes[0, where, :] = moved.astype(jnp.bfloat16)
        if phase == 0:
            moved = jnp.where(column == GRID_W - 1, 0.0, pltpu.roll(values, GRID_W - 1, axis=0))
            planes[5, where, :] = moved.astype(jnp.bfloat16)

    for load in loads[10:13]:
        load.wait()
    for a in range(4):
        for b in range(4):
            tap = a * 4 + b
            block = dot(tile_four, up4[:, tap * c_up : (tap + 1) * c_up]) + up4_b[...]
            for i in range(rows):
                put_row(4 * i + a, b, block[i * GRID_W : (i + 1) * GRID_W])

    half = joined_ref.shape[2] // 2

    def join_rows(phase, first, count):
        windows = [
            planes[phase + col, pl.ds((first + row) * GRID_W, count * GRID_W), :]
            for row in range(3)
            for col in range(3)
        ]
        total = dot(jnp.concatenate(windows, axis=1), join[...])
        for r in range(count):
            for h in range(2):
                joined_f32[first + r, h, pl.ds(phase, GRID_W, stride=4), :] = total[
                    r * GRID_W : (r + 1) * GRID_W, h * half : (h + 1) * half
                ]

    def finish_rows(first, count):
        for r in range(first, first + count):
            for h in range(2):
                joined_ref[r, :, h * half : (h + 1) * half] = joined_f32[r, h].astype(jnp.bfloat16)

    out_rows = 4 * rows
    for phase in range(4):
        join_rows(phase, 1, out_rows - 2)
    finish_rows(1, out_rows - 2)

    tile_two = dot(place, collect(1, recv_two)).astype(jnp.bfloat16)
    for load in loads[13:]:
        load.wait()
    c_two = two_ref.shape[2]
    for a in range(2):
        for b in range(2):
            tap = a * 2 + b
            block = dot(tile_two, up2[:, tap * c_two : (tap + 1) * c_two]) + up2_b[...]
            for i in range(rows):
                for h in range(c_two // 128):
                    two_f32[2 * i + a, h, pl.ds(b, GRID_W, stride=2), :] = block[
                        i * GRID_W : (i + 1) * GRID_W, h * 128 : (h + 1) * 128
                    ]
    for r in range(2 * rows):
        for h in range(c_two // 128):
            two_ref[r, :, h * 128 : (h + 1) * 128] = two_f32[r, h].astype(jnp.bfloat16)

    @pl.when(has_below)
    def _():
        halo(0).wait_send()
        halo(1).wait_recv()

    @pl.when(has_above)
    def _():
        halo(1).wait_send()
        halo(0).wait_recv()

    for side, present, a, row in ((0, has_above, 3, -1), (1, has_below, 0, out_rows)):
        for b in range(4):
            tap = a * 4 + b
            block = dot(edge_in[side], up4[:, tap * c_up : (tap + 1) * c_up]) + up4_b[...]
            put_row(row, b, jnp.where(present, block, 0.0))
    for first in (0, out_rows - 1):
        for phase in range(4):
            join_rows(phase, first, 1)
        finish_rows(first, 1)

    same_rows_ref[...] = collect(2, recv_same)

    for index, send in enumerate((send_four, send_two, send_same)):
        bulk_wait(send, send_sem.at[index])


def write_kernel(joined_ref, two_ref, same_rows_ref, place_ref, joined_out, two_out, same_out, same, sems):
    copies = [
        pltpu.make_async_copy(joined_ref, joined_out, sems.at[0]),
        pltpu.make_async_copy(two_ref, two_out, sems.at[1]),
        pltpu.make_async_copy(same, same_out, sems.at[2]),
    ]
    copies[0].start()
    copies[1].start()
    tile = dot(place_ref[...], same_rows_ref[...]).astype(jnp.bfloat16)
    for i in range(same.shape[0]):
        same[i] = tile[i * GRID_W : (i + 1) * GRID_W]
    copies[2].start()
    for copy in copies:
        copy.wait()


def body(
    hidden_states,
    cell_of,
    proj_four_weight,
    proj_four_bias,
    proj_two_weight,
    proj_two_bias,
    proj_same_weight,
    proj_same_bias,
    up4_weight,
    up4_bias,
    up2_weight,
    up2_bias,
    join_weight,
):
    tok = hidden_states.shape[1]
    shards = lax.axis_size("rows")
    per = tok // shards
    rows = tok // GRID_W
    operands = (
        hidden_states,
        cell_of.reshape(shards, tok),
        proj_four_weight,
        proj_four_bias[None, :],
        proj_two_weight,
        proj_two_bias[None, :],
        proj_same_weight,
        proj_same_bias[None, :],
        up4_weight,
        up4_bias[None, :],
        up2_weight,
        up2_bias[None, :],
        join_weight.reshape(-1, join_weight.shape[3]),
    )
    c_four = proj_four_weight.shape[1]
    c_two = proj_two_weight.shape[1]
    c_same = proj_same_weight.shape[1]
    feat = join_weight.shape[3]
    widths = (c_four, c_two, c_same)
    wire = [pltpu.VMEM((shards, per, c), jnp.bfloat16) for c in widths]
    scratch = [pltpu.VMEM(x.shape, x.dtype) for x in operands]
    scratch += [pltpu.VMEM((tok, max(widths)), jnp.float32)]
    scratch += wire + wire
    scratch += [
        pltpu.VMEM((2, GRID_W, c_four), jnp.bfloat16),
        pltpu.VMEM((2, GRID_W, c_four), jnp.bfloat16),
        pltpu.VMEM((6, (4 * rows + 2) * GRID_W, c_four), jnp.bfloat16),
        pltpu.VMEM((4 * rows, 2, 4 * GRID_W, feat // 2), jnp.float32),
        pltpu.VMEM((2 * rows, c_two // 128, 2 * GRID_W, 128), jnp.float32),
        pltpu.SemaphoreType.DMA((15,)),
        pltpu.SemaphoreType.DMA((3,)),
        pltpu.SemaphoreType.DMA((3,)),
        pltpu.SemaphoreType.DMA((2,)),
        pltpu.SemaphoreType.DMA((2,)),
    ]
    operands = tuple(pltpu.with_memory_space_constraint(x, pltpu.HBM) for x in operands)
    results = pl.pallas_call(
        functools.partial(kernel, shards),
        out_shape=(
            pltpu.VMEM((4 * rows, 4 * GRID_W, feat), jnp.bfloat16),
            pltpu.VMEM((2 * rows, 2 * GRID_W, c_two), jnp.bfloat16),
            pltpu.VMEM((tok, c_same), jnp.bfloat16),
            pltpu.VMEM((tok, tok), jnp.bfloat16),
        ),
        in_specs=[pl.BlockSpec(memory_space=pl.ANY)] * len(operands),
        out_specs=(pl.BlockSpec(memory_space=pltpu.VMEM),) * 4,
        scratch_shapes=scratch,
        compiler_params=pltpu.CompilerParams(
            collective_id=0, has_side_effects=True, vmem_limit_bytes=40 * 1024 * 1024
        ),
    )(*operands)
    results = tuple(pltpu.with_memory_space_constraint(x, pltpu.VMEM) for x in results)
    return pl.pallas_call(
        write_kernel,
        out_shape=(
            jax.ShapeDtypeStruct((4 * rows, 4 * GRID_W, feat), jnp.bfloat16),
            jax.ShapeDtypeStruct((2 * rows, 2 * GRID_W, c_two), jnp.bfloat16),
            jax.ShapeDtypeStruct((rows, GRID_W, c_same), jnp.bfloat16),
        ),
        in_specs=[pl.BlockSpec(memory_space=pltpu.VMEM)] * 4,
        out_specs=(pl.BlockSpec(memory_space=pl.ANY),) * 3,
        scratch_shapes=[
            pltpu.VMEM((rows, GRID_W, c_same), jnp.bfloat16),
            pltpu.SemaphoreType.DMA((3,)),
        ],
        compiler_params=pltpu.CompilerParams(vmem_limit_bytes=8 * 1024 * 1024),
    )(*results)


def solution(mesh):
    rows = P(("img", "rows"), None, None)
    return jax.shard_map(
        body,
        mesh=mesh,
        in_specs=(P(None, ("img", "rows"), None),) + (P(),) * 12,
        out_specs=(rows, rows, rows),
        check_vma=False,
    )
```

profile of v0, /device:TPU:15, one launch (start us, length us, event | category | flops | bytes accessed | tf_op | source)
XLA Modules:
  0.0 18.9 jit_solution(2665506615348213031)
XLA Ops:
  0.6 17.0 %shard_map.148 = (bf16[8,256,256]{2,1,0:T(8,128)(2,1)S(1)}, bf16[4,128,512]{2,1,0:T(8,128)(2,1)S(1)}, bf16[128,1024]{1,0:T(8,128)(2,1)S(1)}, bf16[128,128]{1,0:T(8,128)(2,1)S(1)}) custom-call(bf16[3,128,1024]{2,1,0:T(8,128)(2,1)} %hid_hbm.1, s32[16,128]{1,0:T(8,128)} %bitcast.8, bf16[1024,256]{1,0:T(8,128)(2,1)} %w_four_hbm.1, f32[1,256]{1,0:T(1,128)} %bitcast.12, ...), custom_call_target="tpu_custom_call" | custom-call | tf_op jit(solution)/shard_map/pallas_call | solution.py:366
  17.6 1.2 %shard_map.149 = (bf16[8,256,256]{2,1,0:T(8,128)(2,1)}, bf16[4,128,512]{2,1,0:T(8,128)(2,1)}, bf16[2,64,1024]{2,1,0:T(8,128)(2,1)}) custom-call(bf16[8,256,256]{2,1,0:T(8,128)(2,1)S(1)} %get-tuple-element.7.joined_ref, bf16[4,128,512]{2,1,0:T(8,128)(2,1)S(1)} %get-tuple-element.8.two_ref, bf16[128,1024]{1,0:T(8,128)(2,1)S(1)} %get-tuple-element.9.same_rows_ref, ...), custom_call_target="tpu_custom_call" | custom-call | tf_op jit(solution)/shard_map/pallas_call | solution.py:382
where the time goes:
time: 19.1 us; the launch traced here: 18.9 us
  Pallas kernels  18.2 us (95%)
  between operations  0.64 us (3%)
    pallas_call x1, Pallas kernels, body(): pl.pallas_call(functools.partial(kernel, shards), out_shape=(pltpu.VMEM((...  17 us
    pallas_call x1, Pallas kernels, body(): pl.pallas_call(write_kernel, out_shape=(jax.ShapeDtypeStruct((4 * rows, 4...  1.25 us

commit v1 on v0

--- a/solution.py
+++ b/solution.py
@@ -74,14 +74,18 @@
     recv_sem,
     halo_send_sem,
     halo_recv_sem,
+    relay_sem,
 ):
     me = lax.axis_index("rows")
     img = lax.axis_index("img")
     tok = hid.shape[1]
     per = tok // shards
     rows = tok // GRID_W
-    steps = list(range(1, shards))
-
+    group = shards // 4
+    plane = lax.div(me, group)
+    lower = plane < 2
+    last = plane == 3
+    beside = plane + 1 - 2 * lax.rem(plane, 2)
 
     names = (
         (table_hbm, table),
@@ -102,12 +106,25 @@
     )
     loads = [pltpu.make_async_copy(src, dst, load_sem.at[i]) for i, (src, dst) in enumerate(names)]
 
-    for load in loads[:4]:
+    for load in loads[:10]:
         load.start()
 
+    def row_in(other_plane, i):
+        return partner(me, i) + (other_plane - plane) * group
+
     barrier = pltpu.get_barrier_semaphore()
-    for step in steps:
-        pl.semaphore_signal(barrier, inc=1, device_id=(img, partner(me, step)), device_id_type=MESH)
+
+    def greet(other_plane, some):
+        for i in some:
+            pl.semaphore_signal(barrier, inc=1, device_id=(img, row_in(other_plane, i)), device_id_type=MESH)
+
+    @pl.when(~last)
+    def _():
+        greet(jnp.where(lower, 2, 0), range(group))
+        greet(jnp.where(lower, 3, 1), range(group))
+        greet(beside, range(group))
+
+    greet(plane, range(1, group))
 
     loads[0].wait()
     mine = jnp.broadcast_to(table[pl.ds(me, 1), :].astype(jnp.float32), (tok, tok))
@@ -124,44 +141,108 @@
         projected = (dot(hid[hook], weight[...]) + bias[...]).astype(jnp.bfloat16)
         stage[:, :channels] = dot(scatter, projected)
         if first == 1:
-            for load in loads[4:]:
+            for load in loads[10:]:
                 load.start()
         for shard in range(shards):
             send[shard] = stage[shard * per : (shard + 1) * per, :channels].astype(jnp.bfloat16)
 
-    def exchange(index, send, recv, some):
-        for step in some:
-            other = partner(me, step)
-            pltpu.make_async_remote_copy(
-                src_ref=send.at[other],
-                dst_ref=recv.at[me],
-                send_sem=send_sem.at[index],
-                recv_sem=recv_sem.at[index],
-                device_id=(img, other),
-                device_id_type=MESH,
-            ).start()
-
-    def bulk_wait(buffer, sem):
-        part = buffer.at[pl.ds(0, shards - 1)]
+    def push(index, send, recv, other):
+        pltpu.make_async_remote_copy(
+            src_ref=send.at[other],
+            dst_ref=recv.at[me],
+            send_sem=send_sem.at[index],
+            recv_sem=recv_sem.at[index, plane],
+            device_id=(img, other),
+            device_id_type=MESH,
+        ).start()
+
+    def exchange(index, send, recv, other_plane, some):
+        for i in some:
+            push(index, send, recv, row_in(other_plane, i))
+
+    def exchange_early(index, send, recv):
+        exchange(index, send, recv, jnp.where(lower, 2, 0), range(group))
+
+        @pl.when(~lower)
+        def _():
+            exchange(index, send, recv, 1, range(group))
+
+        @pl.when(plane != 2)
+        def _():
+            exchange(index, send, recv, beside, range(group))
+
+        exchange(index, send, recv, plane, range(1, group))
+        recv[me] = send[me]
+
+    def bulk_wait(buffer, count, sem):
+        part = buffer.at[pl.ds(0, count)]
         pltpu.make_async_copy(part, part, sem).wait()
+
+    def arrive(index, recv, some):
+        for other_plane in some:
+            for mine in (False, True):
+
+                @pl.when((plane == other_plane) == mine)
+                def _():
+                    bulk_wait(recv, group - mine, recv_sem.at[index, other_plane])
 
     def collect(index, recv):
         channels = recv.shape[2]
-        bulk_wait(recv, recv_sem.at[index])
         for shard in range(shards):
             stage[shard * per : (shard + 1) * per, :channels] = recv[shard].astype(jnp.float32)
         return stage[:, :channels].astype(jnp.bfloat16)
 
     project(0, 1, w_four, b_four, send_four)
-    pl.semaphore_wait(barrier, shards - 1)
-    exchange(0, send_four, recv_four, steps)
-    recv_four[me] = send_four[me]
+    pl.semaphore_wait(barrier, jnp.where(last, shards - 1, shards - 1 - group))
+
+    @pl.when(last)
+    def _():
+        for other_plane in (0, 1, 2):
+            to = row_in(other_plane, 0)
+            pl.semaphore_signal(relay_sem, inc=1, device_id=(img, to), device_id_type=MESH)
+
+    exchange_early(0, send_four, recv_four)
     project(1, 4, w_two, b_two, send_two)
-    exchange(1, send_two, recv_two, steps)
-    recv_two[me] = send_two[me]
+    exchange_early(1, send_two, recv_two)
     project(2, 7, w_same, b_same, send_same)
-    far = len(steps) * 3 // 4
-    exchange(2, send_same, recv_same, steps[:far])
+
+    first_rows = range(group // 2)
+    other_rows = range(group // 2, group)
+
+    @pl.when(plane == 1)
+    def _():
+        exchange(2, send_same, recv_same, 2, first_rows)
+
+    @pl.when(~last)
+    def _():
+        pl.semaphore_wait(relay_sem, 1)
+        exchange(0, send_four, recv_four, 3, range(group))
+        exchange(1, send_two, recv_two, 3, range(group))
+
+    spot = lax.rem(me, group)
+    faces_beside = jnp.where(lax.rem(plane, 2) == 0, spot == group - 1, spot == 0)
+    faces_across = ((plane == 1) & (spot == group - 1)) | ((plane == 2) & (spot == 0))
+
+    def exchange_same(after_halo, some):
+        @pl.when((faces_across if after_halo else ~faces_across) & some)
+        def _():
+            exchange(2, send_same, recv_same, jnp.where(lower, 3, 0), range(group))
+
+        @pl.when((faces_beside if after_halo else ~faces_beside) & some)
+        def _():
+            exchange(2, send_same, recv_same, beside, range(group))
+
+        @pl.when((faces_across if after_halo else ~faces_across) & some)
+        def _():
+            exchange(2, send_same, recv_same, jnp.where(lower, 2, 1), other_rows)
+
+            @pl.when(plane != 1)
+            def _():
+                exchange(2, send_same, recv_same, jnp.where(lower, 2, 1), first_rows)
+
+    inner = (plane == 1) | (plane == 2)
+    exchange_same(False, inner)
+    exchange(2, send_same, recv_same, plane, range(1, group))
     recv_same[me] = send_same[me]
 
     wanted = down + me * tok
@@ -174,6 +255,10 @@
     place = (across.astype(jnp.float32) == slot_col).astype(jnp.float32).astype(jnp.bfloat16)
     place_ref[...] = place
 
+    arrive(0, recv_four, (3, 2))
+    exchange_same(False, last)
+    arrive(0, recv_four, (1, 0))
+    exchange_same(False, plane == 0)
     tile_four = dot(place, collect(0, recv_four)).astype(jnp.bfloat16)
     edge_out[0] = tile_four[:GRID_W]
     edge_out[1] = tile_four[tok - GRID_W :]
@@ -199,7 +284,7 @@
     def _():
         halo(1).start()
 
-    exchange(2, send_same, recv_same, steps[far:])
+    exchange_same(True, plane >= 0)
 
     column = lax.broadcasted_iota(jnp.int32, (GRID_W, 1), 0)
     c_up = join.shape[0] // 9
@@ -248,6 +333,7 @@
         join_rows(phase, 1, out_rows - 2)
     finish_rows(1, out_rows - 2)
 
+    arrive(1, recv_two, range(4))
     tile_two = dot(place, collect(1, recv_two)).astype(jnp.bfloat16)
     for load in loads[13:]:
         load.wait()
@@ -285,10 +371,11 @@
             join_rows(phase, first, 1)
         finish_rows(first, 1)
 
+    arrive(2, recv_same, range(4))
     same_rows_ref[...] = collect(2, recv_same)
 
     for index, send in enumerate((send_four, send_two, send_same)):
-        bulk_wait(send, send_sem.at[index])
+        bulk_wait(send, shards - 1, send_sem.at[index])
 
 
 def write_kernel(joined_ref, two_ref, same_rows_ref, place_ref, joined_out, two_out, same_out, same, sems):
@@ -358,9 +445,10 @@
         pltpu.VMEM((2 * rows, c_two // 128, 2 * GRID_W, 128), jnp.float32),
         pltpu.SemaphoreType.DMA((15,)),
         pltpu.SemaphoreType.DMA((3,)),
-        pltpu.SemaphoreType.DMA((3,)),
+        pltpu.SemaphoreType.DMA((3, 4)),
         pltpu.SemaphoreType.DMA((2,)),
         pltpu.SemaphoreType.DMA((2,)),
+        pltpu.SemaphoreType.REGULAR,
     ]
     operands = tuple(pltpu.with_memory_space_constraint(x, pltpu.HBM) for x in operands)
     results = pl.pallas_call(

time: 19.1 us -> 17.8 us (0.932)
  the two profiles are of different devices: /device:TPU:15 before, /device:TPU:1 now
where the time goes in v1:
time: 17.8 us; the launch traced here: 17.6 us
  Pallas kernels  16.9 us (95%)
  between operations  0.64 us (4%)
    pallas_call x1, Pallas kernels, body(): pl.pallas_call(functools.partial(kernel, shards), out_shape=(pltpu.VMEM((...  15.7 us
    pallas_call x1, Pallas kernels, body(): pl.pallas_call(write_kernel, out_shape=(jax.ShapeDtypeStruct((4 * rows, 4...  1.25 us

profile of v1, /device:TPU:1, one launch (start us, length us, event | category | flops | bytes accessed | tf_op | source)
XLA Modules:
  0.0 17.6 jit_solution(1107304224123330261)
XLA Ops:
  0.6 15.7 %shard_map.148 = (bf16[8,256,256]{2,1,0:T(8,128)(2,1)S(1)}, bf16[4,128,512]{2,1,0:T(8,128)(2,1)S(1)}, bf16[128,1024]{1,0:T(8,128)(2,1)S(1)}, bf16[128,128]{1,0:T(8,128)(2,1)S(1)}) custom-call(bf16[3,128,1024]{2,1,0:T(8,128)(2,1)} %hid_hbm.1, s32[16,128]{1,0:T(8,128)} %bitcast.8, bf16[1024,256]{1,0:T(8,128)(2,1)} %w_four_hbm.1, f32[1,256]{1,0:T(1,128)} %bitcast.12, ...), custom_call_target="tpu_custom_call" | custom-call | tf_op jit(solution)/shard_map/pallas_call | solution.py:454
  16.3 1.2 %shard_map.149 = (bf16[8,256,256]{2,1,0:T(8,128)(2,1)}, bf16[4,128,512]{2,1,0:T(8,128)(2,1)}, bf16[2,64,1024]{2,1,0:T(8,128)(2,1)}) custom-call(bf16[8,256,256]{2,1,0:T(8,128)(2,1)S(1)} %get-tuple-element.7.joined_ref, bf16[4,128,512]{2,1,0:T(8,128)(2,1)S(1)} %get-tuple-element.8.two_ref, bf16[128,1024]{1,0:T(8,128)(2,1)S(1)} %get-tuple-element.9.same_rows_ref, ...), custom_call_target="tpu_custom_call" | custom-call | tf_op jit(solution)/shard_map/pallas_call | solution.py:470

commit v2 on v1

--- a/solution.py
+++ b/solution.py
@@ -63,7 +63,7 @@
     send_same,
     recv_four,
     recv_two,
-    recv_same,
+    recv_spare,
     edge_out,
     edge_in,
     planes,
@@ -81,6 +81,10 @@
     tok = hid.shape[1]
     per = tok // shards
     rows = tok // GRID_W
+    block = send_four.shape[1]
+    split = block // per
+    direct = block == 16
+    recv_same = same_rows_ref if direct else recv_spare
     group = shards // 4
     plane = lax.div(me, group)
     lower = plane < 2
@@ -104,7 +108,8 @@
         (up2_hbm, up2),
         (up2_b_hbm, up2_b),
     )
-    loads = [pltpu.make_async_copy(src, dst, load_sem.at[i]) for i, (src, dst) in enumerate(names)]
+    stages = (0, 1, 1, 1, 2, 2, 2, 3, 3, 3, 4, 4, 4, 5, 5)
+    loads = [pltpu.make_async_copy(src, dst, load_sem.at[stage_of]) for (src, dst), stage_of in zip(names, stages)]
 
     for load in loads[:10]:
         load.start()
@@ -132,41 +137,51 @@
     slot_row = jnp.sum(smaller, axis=0, keepdims=True)
     down = lax.broadcasted_iota(jnp.int32, (tok, tok), 0)
     across = lax.broadcasted_iota(jnp.int32, (tok, tok), 1)
-    scatter = (down.astype(jnp.float32) == slot_row).astype(jnp.float32).astype(jnp.bfloat16)
+    shard_row = lax.div(table[pl.ds(me, 1), :], tok).astype(jnp.float32)
+    packed_row = slot_row + shard_row * (block - per)
+    packed_row = jnp.concatenate([packed_row + part * per for part in range(split)], axis=1)
+    packed = lax.broadcasted_iota(jnp.int32, (shards * block, split * tok), 0).astype(jnp.float32)
+    scatter = (packed == packed_row).astype(jnp.float32).astype(jnp.bfloat16)
 
     def project(hook, first, weight, bias, send):
         channels = weight.shape[1]
         for load in loads[first : first + 3]:
             load.wait()
         projected = (dot(hid[hook], weight[...]) + bias[...]).astype(jnp.bfloat16)
-        stage[:, :channels] = dot(scatter, projected)
+        width = channels // split
+        stacked = [projected[:, part * width : (part + 1) * width] for part in range(split)]
+        ordered = dot(scatter, jnp.concatenate(stacked, axis=0))
         if first == 1:
             for load in loads[10:]:
                 load.start()
-        for shard in range(shards):
-            send[shard] = stage[shard * per : (shard + 1) * per, :channels].astype(jnp.bfloat16)
+        if direct:
+            send[...] = ordered.astype(jnp.bfloat16).reshape(send.shape)
+        else:
+            stage[:, :channels] = ordered
+            for shard in range(shards):
+                send[shard] = stage[shard * per : (shard + 1) * per, :channels].astype(jnp.bfloat16)
 
     def push(index, send, recv, other):
         pltpu.make_async_remote_copy(
             src_ref=send.at[other],
             dst_ref=recv.at[me],
-            send_sem=send_sem.at[index],
-            recv_sem=recv_sem.at[index, plane],
+            send_sem=send_sem,
+            recv_sem=recv_sem.at[jnp.where(lower, 0, 1) if index == 0 else index + 1],
             device_id=(img, other),
             device_id_type=MESH,
         ).start()
 
     def exchange(index, send, recv, other_plane, some):
-        for i in some:
+        for i in reversed(some):
             push(index, send, recv, row_in(other_plane, i))
 
     def exchange_early(index, send, recv):
-        exchange(index, send, recv, jnp.where(lower, 2, 0), range(group))
-
         @pl.when(~lower)
         def _():
             exchange(index, send, recv, 1, range(group))
 
+        exchange(index, send, recv, jnp.where(lower, 2, 0), range(group))
+
         @pl.when(plane != 2)
         def _():
             exchange(index, send, recv, beside, range(group))
@@ -178,19 +193,24 @@
         part = buffer.at[pl.ds(0, count)]
         pltpu.make_async_copy(part, part, sem).wait()
 
-    def arrive(index, recv, some):
-        for other_plane in some:
-            for mine in (False, True):
-
-                @pl.when((plane == other_plane) == mine)
-                def _():
-                    bulk_wait(recv, group - mine, recv_sem.at[index, other_plane])
-
-    def collect(index, recv):
-        channels = recv.shape[2]
+    def arrive(recv, planes_in, own, sem):
+        for mine in (0, 1):
+
+            @pl.when(own == (mine == 1))
+            def _():
+                bulk_wait(recv, planes_in * group - mine, recv_sem.at[sem])
+
+    def collect(recv):
+        width = recv.shape[2]
+        if direct:
+            return recv[...].reshape(shards * block, width)
         for shard in range(shards):
-            stage[shard * per : (shard + 1) * per, :channels] = recv[shard].astype(jnp.float32)
-        return stage[:, :channels].astype(jnp.bfloat16)
+            stage[shard * per : (shard + 1) * per, :width] = recv[shard].astype(jnp.float32)
+        return stage[:, :width].astype(jnp.bfloat16)
+
+    def in_cells(recv):
+        tile = dot(place, collect(recv)).astype(jnp.bfloat16)
+        return jnp.concatenate([tile[part * tok : (part + 1) * tok] for part in range(split)], axis=1)
 
     project(0, 1, w_four, b_four, send_four)
     pl.semaphore_wait(barrier, jnp.where(last, shards - 1, shards - 1 - group))
@@ -206,8 +226,8 @@
     exchange_early(1, send_two, recv_two)
     project(2, 7, w_same, b_same, send_same)
 
-    first_rows = range(group // 2)
-    other_rows = range(group // 2, group)
+    other_rows = range(group // 2)
+    first_rows = range(group // 2, group)
 
     @pl.when(plane == 1)
     def _():
@@ -223,16 +243,20 @@
     faces_beside = jnp.where(lax.rem(plane, 2) == 0, spot == group - 1, spot == 0)
     faces_across = ((plane == 1) & (spot == group - 1)) | ((plane == 2) & (spot == 0))
 
+    inner = (plane == 1) | (plane == 2)
+
     def exchange_same(after_halo, some):
-        @pl.when((faces_across if after_halo else ~faces_across) & some)
-        def _():
-            exchange(2, send_same, recv_same, jnp.where(lower, 3, 0), range(group))
+        if not after_halo:
+
+            @pl.when(some)
+            def _():
+                exchange(2, send_same, recv_same, jnp.where(lower, 3, 0), range(group))
 
         @pl.when((faces_beside if after_halo else ~faces_beside) & some)
         def _():
             exchange(2, send_same, recv_same, beside, range(group))
 
-        @pl.when((faces_across if after_halo else ~faces_across) & some)
+        @pl.when((inner if after_halo else ~inner) & some)
         def _():
             exchange(2, send_same, recv_same, jnp.where(lower, 2, 1), other_rows)
 
@@ -240,7 +264,6 @@
             def _():
                 exchange(2, send_same, recv_same, jnp.where(lower, 2, 1), first_rows)
 
-    inner = (plane == 1) | (plane == 2)
     exchange_same(False, inner)
     exchange(2, send_same, recv_same, plane, range(1, group))
     recv_same[me] = send_same[me]
@@ -251,15 +274,17 @@
         source = source + jnp.where(table[shard : shard + 1, :] == wanted, float(shard), 0.0)
     source = jnp.broadcast_to(jnp.sum(source, axis=1, keepdims=True), (tok, tok))
     earlier = jnp.where((source == source.T) & (across < down), 1.0, 0.0)
-    slot_col = source * per + jnp.sum(earlier, axis=1, keepdims=True)
-    place = (across.astype(jnp.float32) == slot_col).astype(jnp.float32).astype(jnp.bfloat16)
+    slot_col = source[:, :1] * block + jnp.sum(earlier, axis=1, keepdims=True)
+    slot_col = jnp.concatenate([slot_col + part * per for part in range(split)], axis=0)
+    packed = lax.broadcasted_iota(jnp.int32, (split * tok, shards * block), 1).astype(jnp.float32)
+    place = (packed == slot_col).astype(jnp.float32).astype(jnp.bfloat16)
     place_ref[...] = place
 
-    arrive(0, recv_four, (3, 2))
+    arrive(recv_four, 2, ~lower, 1)
     exchange_same(False, last)
-    arrive(0, recv_four, (1, 0))
+    arrive(recv_four, 2, lower, 0)
     exchange_same(False, plane == 0)
-    tile_four = dot(place, collect(0, recv_four)).astype(jnp.bfloat16)
+    tile_four = in_cells(recv_four)
     edge_out[0] = tile_four[:GRID_W]
     edge_out[1] = tile_four[tok - GRID_W :]
 
@@ -267,7 +292,7 @@
         return pltpu.make_async_remote_copy(
             src_ref=edge_out.at[1 - side],
             dst_ref=edge_in.at[side],
-            send_sem=halo_send_sem.at[side],
+            send_sem=halo_send_sem,
             recv_sem=halo_recv_sem.at[side],
             device_id=(img, me + 1 if side == 0 else me - 1),
             device_id_type=MESH,
@@ -304,24 +329,32 @@
     for a in range(4):
         for b in range(4):
             tap = a * 4 + b
-            block = dot(tile_four, up4[:, tap * c_up : (tap + 1) * c_up]) + up4_b[...]
+            value = dot(tile_four, up4[:, tap * c_up : (tap + 1) * c_up]) + up4_b[...]
             for i in range(rows):
-                put_row(4 * i + a, b, block[i * GRID_W : (i + 1) * GRID_W])
+                put_row(4 * i + a, b, value[i * GRID_W : (i + 1) * GRID_W])
 
     half = joined_ref.shape[2] // 2
 
-    def join_rows(phase, first, count):
+    def join_rows(jobs, count):
         windows = [
-            planes[phase + col, pl.ds((first + row) * GRID_W, count * GRID_W), :]
-            for row in range(3)
-            for col in range(3)
+            jnp.concatenate(
+                [
+                    planes[phase + col, pl.ds((first + row) * GRID_W, count * GRID_W), :]
+                    for row in range(3)
+                    for col in range(3)
+                ],
+                axis=1,
+            )
+            for phase, first in jobs
         ]
-        total = dot(jnp.concatenate(windows, axis=1), join[...])
-        for r in range(count):
-            for h in range(2):
-                joined_f32[first + r, h, pl.ds(phase, GRID_W, stride=4), :] = total[
-                    r * GRID_W : (r + 1) * GRID_W, h * half : (h + 1) * half
-                ]
+        total = dot(jnp.concatenate(windows, axis=0), join[...])
+        for job, (phase, first) in enumerate(jobs):
+            for r in range(count):
+                at = (job * count + r) * GRID_W
+                for h in range(2):
+                    joined_f32[first + r, h, pl.ds(phase, GRID_W, stride=4), :] = total[
+                        at : at + GRID_W, h * half : (h + 1) * half
+                    ]
 
     def finish_rows(first, count):
         for r in range(first, first + count):
@@ -330,21 +363,21 @@
 
     out_rows = 4 * rows
     for phase in range(4):
-        join_rows(phase, 1, out_rows - 2)
+        join_rows([(phase, 1)], out_rows - 2)
     finish_rows(1, out_rows - 2)
 
-    arrive(1, recv_two, range(4))
-    tile_two = dot(place, collect(1, recv_two)).astype(jnp.bfloat16)
+    bulk_wait(recv_two, shards - 1, recv_sem.at[2])
+    tile_two = in_cells(recv_two)
     for load in loads[13:]:
         load.wait()
     c_two = two_ref.shape[2]
     for a in range(2):
         for b in range(2):
             tap = a * 2 + b
-            block = dot(tile_two, up2[:, tap * c_two : (tap + 1) * c_two]) + up2_b[...]
+            value = dot(tile_two, up2[:, tap * c_two : (tap + 1) * c_two]) + up2_b[...]
             for i in range(rows):
                 for h in range(c_two // 128):
-                    two_f32[2 * i + a, h, pl.ds(b, GRID_W, stride=2), :] = block[
+                    two_f32[2 * i + a, h, pl.ds(b, GRID_W, stride=2), :] = value[
                         i * GRID_W : (i + 1) * GRID_W, h * 128 : (h + 1) * 128
                     ]
     for r in range(2 * rows):
@@ -364,32 +397,38 @@
     for side, present, a, row in ((0, has_above, 3, -1), (1, has_below, 0, out_rows)):
         for b in range(4):
             tap = a * 4 + b
-            block = dot(edge_in[side], up4[:, tap * c_up : (tap + 1) * c_up]) + up4_b[...]
-            put_row(row, b, jnp.where(present, block, 0.0))
-    for first in (0, out_rows - 1):
-        for phase in range(4):
-            join_rows(phase, first, 1)
-        finish_rows(first, 1)
-
-    arrive(2, recv_same, range(4))
-    same_rows_ref[...] = collect(2, recv_same)
-
-    for index, send in enumerate((send_four, send_two, send_same)):
-        bulk_wait(send, shards - 1, send_sem.at[index])
-
-
-def write_kernel(joined_ref, two_ref, same_rows_ref, place_ref, joined_out, two_out, same_out, same, sems):
+            value = dot(edge_in[side], up4[:, tap * c_up : (tap + 1) * c_up]) + up4_b[...]
+            put_row(row, b, jnp.where(present, value, 0.0))
+    join_rows([(phase, first) for first in (0, out_rows - 1) for phase in range(4)], 1)
+    finish_rows(0, 1)
+    finish_rows(out_rows - 1, 1)
+
+    bulk_wait(recv_same, shards - 1, recv_sem.at[3])
+    if not direct:
+        same_rows_ref[...] = collect(recv_same)
+
+    for send in (send_four, send_two, send_same):
+        bulk_wait(send, shards - 1, send_sem)
+
+
+def write_kernel(joined_ref, two_ref, same_rows_ref, place_ref, joined_out, two_out, same_out, same, sem):
     copies = [
-        pltpu.make_async_copy(joined_ref, joined_out, sems.at[0]),
-        pltpu.make_async_copy(two_ref, two_out, sems.at[1]),
-        pltpu.make_async_copy(same, same_out, sems.at[2]),
+        pltpu.make_async_copy(src.at[pl.ds(i, 1)], dst.at[pl.ds(i, 1)], sem)
+        for src, dst in ((joined_ref, joined_out), (two_ref, two_out))
+        for i in range(src.shape[0])
     ]
-    copies[0].start()
-    copies[1].start()
-    tile = dot(place_ref[...], same_rows_ref[...]).astype(jnp.bfloat16)
-    for i in range(same.shape[0]):
-        same[i] = tile[i * GRID_W : (i + 1) * GRID_W]
-    copies[2].start()
+    for copy in copies:
+        copy.start()
+    arrived = same_rows_ref[...]
+    width = arrived.shape[-1]
+    tile = dot(place_ref[...], arrived.reshape(-1, width)).astype(jnp.bfloat16)
+    tok = same.shape[0] * GRID_W
+    for part in range(same.shape[2] // width):
+        for i in range(same.shape[0]):
+            at = part * tok + i * GRID_W
+            same[i, :, part * width : (part + 1) * width] = tile[at : at + GRID_W]
+    copies.append(pltpu.make_async_copy(same, same_out, sem))
+    copies[-1].start()
     for copy in copies:
         copy.wait()
 
@@ -433,20 +472,25 @@
     c_same = proj_same_weight.shape[1]
     feat = join_weight.shape[3]
     widths = (c_four, c_two, c_same)
-    wire = [pltpu.VMEM((shards, per, c), jnp.bfloat16) for c in widths]
+    direct = 16 % per == 0 and all(c * per % (16 * 128) == 0 for c in widths)
+    block = 16 if direct else per
+    split = block // per
+    wire = [pltpu.VMEM((shards, block, c // split), jnp.bfloat16) for c in widths]
+    spare = pltpu.VMEM((8, 128), jnp.bfloat16) if direct else wire[2]
+    arrived = wire[2].shape if direct else (tok, c_same)
     scratch = [pltpu.VMEM(x.shape, x.dtype) for x in operands]
     scratch += [pltpu.VMEM((tok, max(widths)), jnp.float32)]
-    scratch += wire + wire
+    scratch += wire + wire[:2] + [spare]
     scratch += [
         pltpu.VMEM((2, GRID_W, c_four), jnp.bfloat16),
         pltpu.VMEM((2, GRID_W, c_four), jnp.bfloat16),
         pltpu.VMEM((6, (4 * rows + 2) * GRID_W, c_four), jnp.bfloat16),
         pltpu.VMEM((4 * rows, 2, 4 * GRID_W, feat // 2), jnp.float32),
         pltpu.VMEM((2 * rows, c_two // 128, 2 * GRID_W, 128), jnp.float32),
-        pltpu.SemaphoreType.DMA((15,)),
-        pltpu.SemaphoreType.DMA((3,)),
-        pltpu.SemaphoreType.DMA((3, 4)),
-        pltpu.SemaphoreType.DMA((2,)),
+        pltpu.SemaphoreType.DMA((6,)),
+        pltpu.SemaphoreType.DMA,
+        pltpu.SemaphoreType.DMA((4,)),
+        pltpu.SemaphoreType.DMA,
         pltpu.SemaphoreType.DMA((2,)),
         pltpu.SemaphoreType.REGULAR,
     ]
@@ -456,8 +500,8 @@
         out_shape=(
             pltpu.VMEM((4 * rows, 4 * GRID_W, feat), jnp.bfloat16),
             pltpu.VMEM((2 * rows, 2 * GRID_W, c_two), jnp.bfloat16),
-            pltpu.VMEM((tok, c_same), jnp.bfloat16),
-            pltpu.VMEM((tok, tok), jnp.bfloat16),
+            pltpu.VMEM(arrived, jnp.bfloat16),
+            pltpu.VMEM((split * tok, shards * block), jnp.bfloat16),
         ),
         in_specs=[pl.BlockSpec(memory_space=pl.ANY)] * len(operands),
         out_specs=(pl.BlockSpec(memory_space=pltpu.VMEM),) * 4,
@@ -478,7 +522,7 @@
         out_specs=(pl.BlockSpec(memory_space=pl.ANY),) * 3,
         scratch_shapes=[
             pltpu.VMEM((rows, GRID_W, c_same), jnp.bfloat16),
-            pltpu.SemaphoreType.DMA((3,)),
+            pltpu.SemaphoreType.DMA,
         ],
         compiler_params=pltpu.CompilerParams(vmem_limit_bytes=8 * 1024 * 1024),
     )(*results)

time: 17.8 us -> 17.2 us (0.966)
  the two profiles are of different devices: /device:TPU:1 before, /device:TPU:0 now
where the time goes in v2:
time: 17.2 us; the launch traced here: 17 us
  Pallas kernels  16.3 us (95%)
  between operations  0.64 us (4%)
    pallas_call x1, Pallas kernels, body(): pl.pallas_call(functools.partial(kernel, shards), out_shape=(pltpu.VMEM((...  15.1 us
    pallas_call x1, Pallas kernels, body(): pl.pallas_call(write_kernel, out_shape=(jax.ShapeDtypeStruct((4 * rows, 4...  1.24 us

profile of v2, /device:TPU:0, one launch (start us, length us, event | category | flops | bytes accessed | tf_op | source)
XLA Modules:
  0.0 17.0 jit_solution(17340072369511565848)
XLA Ops:
  0.6 15.1 %shard_map.148 = (bf16[8,256,256]{2,1,0:T(8,128)(2,1)S(1)}, bf16[4,128,512]{2,1,0:T(8,128)(2,1)S(1)}, bf16[16,16,512]{2,1,0:T(8,128)(2,1)S(1)}, bf16[256,256]{1,0:T(8,128)(2,1)S(1)}) custom-call(bf16[3,128,1024]{2,1,0:T(8,128)(2,1)} %hid_hbm.1, s32[16,128]{1,0:T(8,128)} %bitcast.8, bf16[1024,256]{1,0:T(8,128)(2,1)} %w_four_hbm.1, f32[1,256]{1,0:T(1,128)} %bitcast.12, ...), custom_call_target="tpu_custom_call" | custom-call | tf_op jit(solution)/shard_map/pallas_call | solution.py:498
  15.7 1.2 %shard_map.149 = (bf16[8,256,256]{2,1,0:T(8,128)(2,1)}, bf16[4,128,512]{2,1,0:T(8,128)(2,1)}, bf16[2,64,1024]{2,1,0:T(8,128)(2,1)}) custom-call(bf16[8,256,256]{2,1,0:T(8,128)(2,1)S(1)} %get-tuple-element.7.joined_ref, bf16[4,128,512]{2,1,0:T(8,128)(2,1)S(1)} %get-tuple-element.8.two_ref, bf16[16,16,512]{2,1,0:T(8,128)(2,1)S(1)} %get-tuple-element.9.same_rows_ref, ...), custom_call_target="tpu_custom_call" | custom-call | tf_op jit(solution)/shard_map/pallas_call | solution.py:514

commit v3 on v2

--- a/solution.py
+++ b/solution.py
@@ -108,10 +108,10 @@
         (up2_hbm, up2),
         (up2_b_hbm, up2_b),
     )
-    stages = (0, 1, 1, 1, 2, 2, 2, 3, 3, 3, 4, 4, 4, 5, 5)
+    stages = (0, 1, 1, 1, 2, 2, 2, 3, 3, 3, 4, 4, 4, 4, 4)
     loads = [pltpu.make_async_copy(src, dst, load_sem.at[stage_of]) for (src, dst), stage_of in zip(names, stages)]
 
-    for load in loads[:10]:
+    for load in loads[:4]:
         load.start()
 
     def row_in(other_plane, i):
@@ -130,6 +130,9 @@
         greet(beside, range(group))
 
     greet(plane, range(1, group))
+
+    for load in loads[4:10]:
+        load.start()
 
     loads[0].wait()
     mine = jnp.broadcast_to(table[pl.ds(me, 1), :].astype(jnp.float32), (tok, tok))
@@ -176,11 +179,11 @@
             push(index, send, recv, row_in(other_plane, i))
 
     def exchange_early(index, send, recv):
+        exchange(index, send, recv, jnp.where(lower, 2, 0), range(group))
+
         @pl.when(~lower)
         def _():
             exchange(index, send, recv, 1, range(group))
-
-        exchange(index, send, recv, jnp.where(lower, 2, 0), range(group))
 
         @pl.when(plane != 2)
         def _():
@@ -213,18 +216,37 @@
         return jnp.concatenate([tile[part * tok : (part + 1) * tok] for part in range(split)], axis=1)
 
     project(0, 1, w_four, b_four, send_four)
-    pl.semaphore_wait(barrier, jnp.where(last, shards - 1, shards - 1 - group))
-
-    @pl.when(last)
-    def _():
-        for other_plane in (0, 1, 2):
-            to = row_in(other_plane, 0)
-            pl.semaphore_signal(relay_sem, inc=1, device_id=(img, to), device_id_type=MESH)
-
-    exchange_early(0, send_four, recv_four)
+
+    @pl.when(plane >= 2)
+    def _():
+        pl.semaphore_wait(barrier, jnp.where(last, shards - 1, shards - 1 - group))
+
+        @pl.when(last)
+        def _():
+            for other_plane in (0, 1, 2):
+                to = row_in(other_plane, 0)
+                pl.semaphore_signal(relay_sem, inc=1, device_id=(img, to), device_id_type=MESH)
+
+        exchange_early(0, send_four, recv_four)
+
     project(1, 4, w_two, b_two, send_two)
-    exchange_early(1, send_two, recv_two)
+
+    @pl.when(plane == 1)
+    def _():
+        pl.semaphore_wait(barrier, shards - 1 - group)
+        exchange_early(0, send_four, recv_four)
+
+    @pl.when(plane > 0)
+    def _():
+        exchange_early(1, send_two, recv_two)
+
     project(2, 7, w_same, b_same, send_same)
+
+    @pl.when(plane == 0)
+    def _():
+        pl.semaphore_wait(barrier, shards - 1 - group)
+        exchange_early(0, send_four, recv_four)
+        exchange_early(1, send_two, recv_two)
 
     other_rows = range(group // 2)
     first_rows = range(group // 2, group)
@@ -241,30 +263,32 @@
 
     spot = lax.rem(me, group)
     faces_beside = jnp.where(lax.rem(plane, 2) == 0, spot == group - 1, spot == 0)
+
+    inner = (plane == 1) | (plane == 2)
+    outer = ~inner
     faces_across = ((plane == 1) & (spot == group - 1)) | ((plane == 2) & (spot == 0))
 
-    inner = (plane == 1) | (plane == 2)
-
-    def exchange_same(after_halo, some):
-        if not after_halo:
-
-            @pl.when(some)
-            def _():
-                exchange(2, send_same, recv_same, jnp.where(lower, 3, 0), range(group))
-
-        @pl.when((faces_beside if after_halo else ~faces_beside) & some)
+    def same_far(some, rows_to=range(group)):
+        @pl.when(some)
+        def _():
+            exchange(2, send_same, recv_same, jnp.where(lower, 3, 0), rows_to)
+
+    def same_beside(some):
+        @pl.when(some)
         def _():
             exchange(2, send_same, recv_same, beside, range(group))
 
-        @pl.when((inner if after_halo else ~inner) & some)
+    def same_across(some):
+        @pl.when(some & (plane != 1))
+        def _():
+            exchange(2, send_same, recv_same, jnp.where(lower, 2, 1), first_rows)
+
+        @pl.when(some)
         def _():
             exchange(2, send_same, recv_same, jnp.where(lower, 2, 1), other_rows)
 
-            @pl.when(plane != 1)
-            def _():
-                exchange(2, send_same, recv_same, jnp.where(lower, 2, 1), first_rows)
-
-    exchange_same(False, inner)
+    same_far(inner)
+    same_beside(inner)
     exchange(2, send_same, recv_same, plane, range(1, group))
     recv_same[me] = send_same[me]
 
@@ -281,9 +305,14 @@
     place_ref[...] = place
 
     arrive(recv_four, 2, ~lower, 1)
-    exchange_same(False, last)
+    same_far(last)
+    same_beside(last & ~faces_beside)
+    same_across(last)
     arrive(recv_four, 2, lower, 0)
-    exchange_same(False, plane == 0)
+    free = (plane == 0) & ~faces_beside
+    same_far(free)
+    same_beside(free)
+    same_across(free)
     tile_four = in_cells(recv_four)
     edge_out[0] = tile_four[:GRID_W]
     edge_out[1] = tile_four[tok - GRID_W :]
@@ -309,7 +338,10 @@
     def _():
         halo(1).start()
 
-    exchange_same(True, plane >= 0)
+    facing = (plane == 0) & faces_beside
+    same_far(facing)
+    same_beside(outer & faces_beside)
+    same_across(inner | facing)
 
     column = lax.broadcasted_iota(jnp.int32, (GRID_W, 1), 0)
     c_up = join.shape[0] // 9
@@ -324,7 +356,7 @@
             moved = jnp.where(column == GRID_W - 1, 0.0, pltpu.roll(values, GRID_W - 1, axis=0))
             planes[5, where, :] = moved.astype(jnp.bfloat16)
 
-    for load in loads[10:13]:
+    for load in loads[10:]:
         load.wait()
     for a in range(4):
         for b in range(4):
@@ -368,8 +400,6 @@
 
     bulk_wait(recv_two, shards - 1, recv_sem.at[2])
     tile_two = in_cells(recv_two)
-    for load in loads[13:]:
-        load.wait()
     c_two = two_ref.shape[2]
     for a in range(2):
         for b in range(2):
@@ -487,7 +517,7 @@
         pltpu.VMEM((6, (4 * rows + 2) * GRID_W, c_four), jnp.bfloat16),
         pltpu.VMEM((4 * rows, 2, 4 * GRID_W, feat // 2), jnp.float32),
         pltpu.VMEM((2 * rows, c_two // 128, 2 * GRID_W, 128), jnp.float32),
-        pltpu.SemaphoreType.DMA((6,)),
+        pltpu.SemaphoreType.DMA((5,)),
         pltpu.SemaphoreType.DMA,
         pltpu.SemaphoreType.DMA((4,)),
         pltpu.SemaphoreType.DMA,

time: 17.2 us -> 17 us (0.988)
  the two profiles are of different devices: /device:TPU:0 before, /device:TPU:15 now
where the time goes in v3:
time: 17 us; the launch traced here: 16.8 us
  Pallas kernels  16.2 us (95%)
  between operations  0.64 us (4%)
    pallas_call x1, Pallas kernels, body(): pl.pallas_call(functools.partial(kernel, shards), out_shape=(pltpu.VMEM((...  14.9 us
    pallas_call x1, Pallas kernels, body(): pl.pallas_call(write_kernel, out_shape=(jax.ShapeDtypeStruct((4 * rows, 4...  1.24 us

profile of v3, /device:TPU:15, one launch (start us, length us, event | category | flops | bytes accessed | tf_op | source)
XLA Modules:
  0.0 16.8 jit_solution(17554609202991044346)
XLA Ops:
  0.6 14.9 %shard_map.148 = (bf16[8,256,256]{2,1,0:T(8,128)(2,1)S(1)}, bf16[4,128,512]{2,1,0:T(8,128)(2,1)S(1)}, bf16[16,16,512]{2,1,0:T(8,128)(2,1)S(1)}, bf16[256,256]{1,0:T(8,128)(2,1)S(1)}) custom-call(bf16[3,128,1024]{2,1,0:T(8,128)(2,1)} %hid_hbm.1, s32[16,128]{1,0:T(8,128)} %bitcast.8, bf16[1024,256]{1,0:T(8,128)(2,1)} %w_four_hbm.1, f32[1,256]{1,0:T(1,128)} %bitcast.12, ...), custom_call_target="tpu_custom_call" | custom-call | tf_op jit(solution)/shard_map/pallas_call | solution.py:528
  15.6 1.2 %shard_map.149 = (bf16[8,256,256]{2,1,0:T(8,128)(2,1)}, bf16[4,128,512]{2,1,0:T(8,128)(2,1)}, bf16[2,64,1024]{2,1,0:T(8,128)(2,1)}) custom-call(bf16[8,256,256]{2,1,0:T(8,128)(2,1)S(1)} %get-tuple-element.7.joined_ref, bf16[4,128,512]{2,1,0:T(8,128)(2,1)S(1)} %get-tuple-element.8.two_ref, bf16[16,16,512]{2,1,0:T(8,128)(2,1)S(1)} %get-tuple-element.9.same_rows_ref, ...), custom_call_target="tpu_custom_call" | custom-call | tf_op jit(solution)/shard_map/pallas_call | solution.py:544

commit v4 on v3

--- a/solution.py
+++ b/solution.py
@@ -67,6 +67,7 @@
     edge_out,
     edge_in,
     planes,
+    edge_sum,
     joined_f32,
     two_f32,
     load_sem,
@@ -289,6 +290,7 @@
 
     same_far(inner)
     same_beside(inner)
+    same_across(inner & ~faces_across)
     exchange(2, send_same, recv_same, plane, range(1, group))
     recv_same[me] = send_same[me]
 
@@ -341,7 +343,7 @@
     facing = (plane == 0) & faces_beside
     same_far(facing)
     same_beside(outer & faces_beside)
-    same_across(inner | facing)
+    same_across(faces_across | facing)
 
     column = lax.broadcasted_iota(jnp.int32, (GRID_W, 1), 0)
     c_up = join.shape[0] // 9
@@ -414,6 +416,25 @@
         for h in range(c_two // 128):
             two_ref[r, :, h * 128 : (h + 1) * 128] = two_f32[r, h].astype(jnp.bfloat16)
 
+    def edge_product(first, tap_rows):
+        windows = [
+            jnp.concatenate(
+                [
+                    planes[phase + col, pl.ds((first + row) * GRID_W, GRID_W), :]
+                    for row in tap_rows
+                    for col in range(3)
+                ],
+                axis=1,
+            )
+            for phase in range(4)
+        ]
+        weights = join[tap_rows[0] * 3 * c_up : (tap_rows[-1] + 1) * 3 * c_up, :]
+        return dot(jnp.concatenate(windows, axis=0), weights)
+
+    borders = ((0, (1, 2), (0,)), (out_rows - 1, (0, 1), (2,)))
+    for side, (first, inside, beyond) in enumerate(borders):
+        edge_sum[side] = edge_product(first, inside)
+
     @pl.when(has_below)
     def _():
         halo(0).wait_send()
@@ -429,7 +450,13 @@
             tap = a * 4 + b
             value = dot(edge_in[side], up4[:, tap * c_up : (tap + 1) * c_up]) + up4_b[...]
             put_row(row, b, jnp.where(present, value, 0.0))
-    join_rows([(phase, first) for first in (0, out_rows - 1) for phase in range(4)], 1)
+    for side, (first, inside, beyond) in enumerate(borders):
+        total = edge_sum[side] + edge_product(first, beyond)
+        for phase in range(4):
+            for h in range(2):
+                joined_f32[first, h, pl.ds(phase, GRID_W, stride=4), :] = total[
+                    phase * GRID_W : (phase + 1) * GRID_W, h * half : (h + 1) * half
+                ]
     finish_rows(0, 1)
     finish_rows(out_rows - 1, 1)
 
@@ -515,6 +542,7 @@
         pltpu.VMEM((2, GRID_W, c_four), jnp.bfloat16),
         pltpu.VMEM((2, GRID_W, c_four), jnp.bfloat16),
         pltpu.VMEM((6, (4 * rows + 2) * GRID_W, c_four), jnp.bfloat16),
+        pltpu.VMEM((2, 4 * GRID_W, feat), jnp.float32),
         pltpu.VMEM((4 * rows, 2, 4 * GRID_W, feat // 2), jnp.float32),
         pltpu.VMEM((2 * rows, c_two // 128, 2 * GRID_W, 128), jnp.float32),
         pltpu.SemaphoreType.DMA((5,)),

time: 17 us -> 16.9 us (level)
  the two profiles are of different devices: /device:TPU:15 before, /device:TPU:11 now
where the time goes in v4:
time: 16.9 us; the launch traced here: 16.7 us
  Pallas kernels  16.1 us (95%)
  between operations  0.64 us (4%)
    pallas_call x1, Pallas kernels, body(): pl.pallas_call(functools.partial(kernel, shards), out_shape=(pltpu.VMEM((...  14.8 us
    pallas_call x1, Pallas kernels, body(): pl.pallas_call(write_kernel, out_shape=(jax.ShapeDtypeStruct((4 * rows, 4...  1.24 us

profile of v4, /device:TPU:11, one launch (start us, length us, event | category | flops | bytes accessed | tf_op | source)
XLA Modules:
  0.0 16.7 jit_solution(16127236814180188648)
XLA Ops:
  0.6 14.8 %shard_map.148 = (bf16[8,256,256]{2,1,0:T(8,128)(2,1)S(1)}, bf16[4,128,512]{2,1,0:T(8,128)(2,1)S(1)}, bf16[16,16,512]{2,1,0:T(8,128)(2,1)S(1)}, bf16[256,256]{1,0:T(8,128)(2,1)S(1)}) custom-call(bf16[3,128,1024]{2,1,0:T(8,128)(2,1)} %hid_hbm.1, s32[16,128]{1,0:T(8,128)} %bitcast.8, bf16[1024,256]{1,0:T(8,128)(2,1)} %w_four_hbm.1, f32[1,256]{1,0:T(1,128)} %bitcast.12, ...), custom_call_target="tpu_custom_call" | custom-call | tf_op jit(solution)/shard_map/pallas_call | solution.py:556
  15.5 1.2 %shard_map.149 = (bf16[8,256,256]{2,1,0:T(8,128)(2,1)}, bf16[4,128,512]{2,1,0:T(8,128)(2,1)}, bf16[2,64,1024]{2,1,0:T(8,128)(2,1)}) custom-call(bf16[8,256,256]{2,1,0:T(8,128)(2,1)S(1)} %get-tuple-element.7.joined_ref, bf16[4,128,512]{2,1,0:T(8,128)(2,1)S(1)} %get-tuple-element.8.two_ref, bf16[16,16,512]{2,1,0:T(8,128)(2,1)S(1)} %get-tuple-element.9.same_rows_ref, ...), custom_call_target="tpu_custom_call" | custom-call | tf_op jit(solution)/shard_map/pallas_call | solution.py:572

commit v5 on v4

--- a/solution.py
+++ b/solution.py
@@ -308,7 +308,7 @@
 
     arrive(recv_four, 2, ~lower, 1)
     same_far(last)
-    same_beside(last & ~faces_beside)
+    same_beside(last)
     same_across(last)
     arrive(recv_four, 2, lower, 0)
     free = (plane == 0) & ~faces_beside
@@ -342,7 +342,7 @@
 
     facing = (plane == 0) & faces_beside
     same_far(facing)
-    same_beside(outer & faces_beside)
+    same_beside((plane == 0) & faces_beside)
     same_across(faces_across | facing)
 
     column = lax.broadcasted_iota(jnp.int32, (GRID_W, 1), 0)

time: 16.9 us -> 16.9 us (level)
  no operation moved by 1% of the time
where the time goes in v5:
time: 16.9 us; the launch traced here: 16.7 us
  Pallas kernels  16.1 us (95%)
  between operations  0.64 us (4%)
    pallas_call x1, Pallas kernels, body(): pl.pallas_call(functools.partial(kernel, shards), out_shape=(pltpu.VMEM((...  14.8 us
    pallas_call x1, Pallas kernels, body(): pl.pallas_call(write_kernel, out_shape=(jax.ShapeDtypeStruct((4 * rows, 4...  1.24 us

profile of v5, /device:TPU:11, one launch (start us, length us, event | category | flops | bytes accessed | tf_op | source)
XLA Modules:
  0.0 16.7 jit_solution(3946963976802175060)
XLA Ops:
  0.6 14.8 %shard_map.148 = (bf16[8,256,256]{2,1,0:T(8,128)(2,1)S(1)}, bf16[4,128,512]{2,1,0:T(8,128)(2,1)S(1)}, bf16[16,16,512]{2,1,0:T(8,128)(2,1)S(1)}, bf16[256,256]{1,0:T(8,128)(2,1)S(1)}) custom-call(bf16[3,128,1024]{2,1,0:T(8,128)(2,1)} %hid_hbm.1, s32[16,128]{1,0:T(8,128)} %bitcast.8, bf16[1024,256]{1,0:T(8,128)(2,1)} %w_four_hbm.1, f32[1,256]{1,0:T(1,128)} %bitcast.12, ...), custom_call_target="tpu_custom_call" | custom-call | tf_op jit(solution)/shard_map/pallas_call | solution.py:556
  15.5 1.2 %shard_map.149 = (bf16[8,256,256]{2,1,0:T(8,128)(2,1)}, bf16[4,128,512]{2,1,0:T(8,128)(2,1)}, bf16[2,64,1024]{2,1,0:T(8,128)(2,1)}) custom-call(bf16[8,256,256]{2,1,0:T(8,128)(2,1)S(1)} %get-tuple-element.7.joined_ref, bf16[4,128,512]{2,1,0:T(8,128)(2,1)S(1)} %get-tuple-element.8.two_ref, bf16[16,16,512]{2,1,0:T(8,128)(2,1)S(1)} %get-tuple-element.9.same_rows_ref, ...), custom_call_target="tpu_custom_call" | custom-call | tf_op jit(solution)/shard_map/pallas_call | solution.py:572

commit v6 on v5

--- a/solution.py
+++ b/solution.py
@@ -73,7 +73,6 @@
     load_sem,
     send_sem,
     recv_sem,
-    halo_send_sem,
     halo_recv_sem,
     relay_sem,
 ):
@@ -109,7 +108,7 @@
         (up2_hbm, up2),
         (up2_b_hbm, up2_b),
     )
-    stages = (0, 1, 1, 1, 2, 2, 2, 3, 3, 3, 4, 4, 4, 4, 4)
+    stages = (0, 1, 1, 1, 2, 2, 2, 3, 3, 3, 0, 0, 0, 0, 0)
     loads = [pltpu.make_async_copy(src, dst, load_sem.at[stage_of]) for (src, dst), stage_of in zip(names, stages)]
 
     for load in loads[:4]:
@@ -323,7 +322,7 @@
         return pltpu.make_async_remote_copy(
             src_ref=edge_out.at[1 - side],
             dst_ref=edge_in.at[side],
-            send_sem=halo_send_sem,
+            send_sem=send_sem,
             recv_sem=halo_recv_sem.at[side],
             device_id=(img, me + 1 if side == 0 else me - 1),
             device_id_type=MESH,
@@ -437,12 +436,10 @@
 
     @pl.when(has_below)
     def _():
-        halo(0).wait_send()
         halo(1).wait_recv()
 
     @pl.when(has_above)
     def _():
-        halo(1).wait_send()
         halo(0).wait_recv()
 
     for side, present, a, row in ((0, has_above, 3, -1), (1, has_below, 0, out_rows)):
@@ -466,6 +463,14 @@
 
     for send in (send_four, send_two, send_same):
         bulk_wait(send, shards - 1, send_sem)
+
+    @pl.when(has_below)
+    def _():
+        halo(0).wait_send()
+
+    @pl.when(has_above)
+    def _():
+        halo(1).wait_send()
 
 
 def write_kernel(joined_ref, two_ref, same_rows_ref, place_ref, joined_out, two_out, same_out, same, sem):
@@ -545,10 +550,9 @@
         pltpu.VMEM((2, 4 * GRID_W, feat), jnp.float32),
         pltpu.VMEM((4 * rows, 2, 4 * GRID_W, feat // 2), jnp.float32),
         pltpu.VMEM((2 * rows, c_two // 128, 2 * GRID_W, 128), jnp.float32),
-        pltpu.SemaphoreType.DMA((5,)),
+        pltpu.SemaphoreType.DMA((4,)),
         pltpu.SemaphoreType.DMA,
         pltpu.SemaphoreType.DMA((4,)),
-        pltpu.SemaphoreType.DMA,
         pltpu.SemaphoreType.DMA((2,)),
         pltpu.SemaphoreType.REGULAR,
     ]

time: 16.9 us -> 16.9 us (level)
  no operation moved by 1% of the time
where the time goes in v6:
time: 16.9 us; the launch traced here: 16.7 us
  Pallas kernels  16 us (95%)
  between operations  0.64 us (4%)
    pallas_call x1, Pallas kernels, body(): pl.pallas_call(functools.partial(kernel, shards), out_shape=(pltpu.VMEM((...  14.8 us
    pallas_call x1, Pallas kernels, body(): pl.pallas_call(write_kernel, out_shape=(jax.ShapeDtypeStruct((4 * rows, 4...  1.24 us

profile of v6, /device:TPU:11, one launch (start us, length us, event | category | flops | bytes accessed | tf_op | source)
XLA Modules:
  0.0 16.7 jit_solution(10715110970161941462)
XLA Ops:
  0.6 14.8 %shard_map.148 = (bf16[8,256,256]{2,1,0:T(8,128)(2,1)S(1)}, bf16[4,128,512]{2,1,0:T(8,128)(2,1)S(1)}, bf16[16,16,512]{2,1,0:T(8,128)(2,1)S(1)}, bf16[256,256]{1,0:T(8,128)(2,1)S(1)}) custom-call(bf16[3,128,1024]{2,1,0:T(8,128)(2,1)} %hid_hbm.1, s32[16,128]{1,0:T(8,128)} %bitcast.8, bf16[1024,256]{1,0:T(8,128)(2,1)} %w_four_hbm.1, f32[1,256]{1,0:T(1,128)} %bitcast.12, ...), custom_call_target="tpu_custom_call" | custom-call | tf_op jit(solution)/shard_map/pallas_call | solution.py:560
  15.4 1.2 %shard_map.149 = (bf16[8,256,256]{2,1,0:T(8,128)(2,1)}, bf16[4,128,512]{2,1,0:T(8,128)(2,1)}, bf16[2,64,1024]{2,1,0:T(8,128)(2,1)}) custom-call(bf16[8,256,256]{2,1,0:T(8,128)(2,1)S(1)} %get-tuple-element.7.joined_ref, bf16[4,128,512]{2,1,0:T(8,128)(2,1)S(1)} %get-tuple-element.8.two_ref, bf16[16,16,512]{2,1,0:T(8,128)(2,1)S(1)} %get-tuple-element.9.same_rows_ref, ...), custom_call_target="tpu_custom_call" | custom-call | tf_op jit(solution)/shard_map/pallas_call | solution.py:576
